TPU v7x, 256 devices: a whole 4x4x8 slice. The times are simulated.
256 devices in a mesh: ep: 64 (over z, y, core), fsdp: 4 (over x).
Axes of the slice: x: 4, y: 4, z: 8, core: 2. Of those that a mesh axis runs over, the one named last changes fastest.
Arguments:
- train_gate: float32 [64, 2048, 1024], P('ep', 'fsdp'), may hold values from -0.1875 to 0.1875
- other_gate: bfloat16 [64, 2048, 1024], P('ep', 'fsdp'), may hold values from -0.0625 to 0.0625
- train_up: float32 [64, 2048, 1024], P('ep', 'fsdp'), may hold values from -0.1875 to 0.1875
- other_up: bfloat16 [64, 2048, 1024], P('ep', 'fsdp'), may hold values from -0.0625 to 0.0625
- router_weight: float32 [2048, 64], P('fsdp', 'ep'), may hold values from -0.125 to 0.125
- router_gain: float32 [2048], P('fsdp'), may hold values from 0.25 to 1.75
Outputs:
- ready_gate: bfloat16 [64, 2048, 1024], P('ep')
- ready_up: bfloat16 [64, 2048, 1024], P('ep')
- scale_gate: float32 [64, 1024], P('ep')
- scale_up: float32 [64, 1024], P('ep')
- serve_router: bfloat16 [2048, 64], replicated
All inputs are finite; a program needn't handle non-finite values.
Results may differ from a plain program's by a relative error of at most 0.001.
Values may be sent and summed in bfloat16 or wider, within the bound.
A program may use at most 64 MiB of HBM per device.

v0:
```python
import jax
import jax.numpy as jnp
from jax import lax
from jax.sharding import PartitionSpec as P


def copy_for_each(value, axis):
    copies = jnp.broadcast_to(value, (lax.axis_size(axis), *value.shape))
    return lax.all_to_all(copies, axis, split_axis=0, concat_axis=0, tiled=True)


def over_copies(value, axis):
    return copy_for_each(value, axis).sum(axis=0)


def packed_total(arrays, axis):
    flat, at, outs = (jnp.concatenate([a.reshape(-1) for a in arrays]), 0, [])
    so_far = over_copies(flat, axis)
    for a in arrays:
        outs.append(so_far[at : at + a.size].reshape(a.shape))
        at += a.size
    return tuple(outs)


def side_by_side(arrays, axis, dim, along):
    widths = [a.shape[along] for a in arrays]
    both = jnp.concatenate(arrays, axis=along)
    out = lax.all_gather(both, axis, axis=dim, tiled=True)
    return tuple(jnp.split(out, [sum(widths[:k]) for k in range(1, len(widths))], axis=along))


def joined_along(blocks, dim):
    dims = list(blocks.shape[1:])
    dims[dim] *= blocks.shape[0]
    return jnp.moveaxis(blocks, 0, dim).reshape(dims)


def gather_directly(value, axis, dim):
    return joined_along(copy_for_each(value, axis), dim)


def body(train_gate, other_gate, train_up, other_up, router_weight, router_gain):
    latest_gate = train_gate + other_gate.astype(jnp.float32)
    latest_up = train_up + other_up.astype(jnp.float32)
    total_gate, total_up = packed_total(
        (jnp.sum(latest_gate * latest_gate, axis=1), jnp.sum(latest_up * latest_up, axis=1)), "fsdp"
    )
    scale_gate = jnp.sqrt(total_gate)
    scale_up = jnp.sqrt(total_up)
    narrow_gate, narrow_up = (
        (latest_gate / jnp.expand_dims(scale_gate, 1)).astype(jnp.bfloat16),
        (latest_up / jnp.expand_dims(scale_up, 1)).astype(jnp.bfloat16),
    )
    ready_gate, ready_up = side_by_side((narrow_gate, narrow_up), "fsdp", 1, 0)
    part_router = (router_weight * router_gain[:, None]).astype(jnp.bfloat16)
    row_router = lax.all_gather(part_router, "fsdp", axis=0, tiled=True)
    serve_router = gather_directly(row_router, "ep", 1)
    return (ready_gate, ready_up, scale_gate, scale_up, serve_router)


def solution(mesh):
    placed = (
        P("ep", "fsdp", None),
        P("ep", "fsdp", None),
        P("ep", "fsdp", None),
        P("ep", "fsdp", None),
        P("fsdp", "ep"),
        P("fsdp"),
    )
    return jax.shard_map(
        body,
        mesh=mesh,
        in_specs=placed,
        out_specs=(P("ep", None, None), P("ep", None, None), P("ep", None), P("ep", None), P()),
        check_vma=False,
    )
```

profile of v0, /device:TPU:1, one launch (start us, length us, event | category | flops | bytes accessed | tf_op | source)
XLA Modules:
  0.0 124.7 jit_solution(4241068722860294294)
XLA Ops:
  7.2 0.0 copy-start
  7.2 0.0 copy-start.2
  7.2 0.0 all-gather.2.cloned.1.call-start
  7.2 3.6 %multiply_reduce_fusion = (f32[1024]{0:T(1024)S(1)}, f32[1024]{0:T(1024)S(1)}) fusion(f32[1,512,1024]{2,1,0:T(8,128)} %param.8, bf16[1,512,1024]{2,1,0:T(8,128)(2,1)} %param.9, f32[1,512,1024]{2,1,0:T(8,128)} %param.6, bf16[1,512,1024]{2,1,0:T(8,128)(2,1)} %param.7), kind=kLoop, calls=%fused_computation.3 | loop fusion | flops 4192256 | bytes 6299648 | tf_op jit(solution)/shard_map/reduce_sum | solution.py:46
  10.9 8.9 %all_to_all.11 = f32[4,1,2048]{2,1,0:T(1,128)S(1)} all-to-all(f32[4,1,2048]{2,1,0:T(1,128)S(1)} %broadcast_in_dim.11), channel_id=1, replica_groups=mesh['ep'=64,'fsdp'=4] {'fsdp'}, dimensions={0} | all-to-all | bytes 65536 | tf_op jit(solution)/shard_map/all_to_all | solution.py:9
  19.9 0.0 copy-start.5
  19.9 0.0 copy-start.4
  19.9 0.0 copy-done
  19.9 0.0 copy-done.2
  19.9 0.0 copy-start.1
  19.9 0.0 copy-start.3
  20.0 0.4 divide_convert_fusion
  20.3 0.1 copy-done.5
  20.5 0.0 copy-done.4
  20.5 1.0 copy-done.1
  21.5 0.3 copy-done.3
  21.8 0.4 divide_convert_fusion.1
  22.2 1.5 %pad_maximum_fusion = bf16[2,512,1024]{2,1,0:T(8,128)(2,1)} fusion(bf16[1,512,1024]{2,1,0:T(8,128)(2,1)S(1)} %divide_convert_fusion, bf16[1,512,1024]{2,1,0:T(8,128)(2,1)S(1)} %divide_convert_fusion.1), kind=kLoop, calls=%fused_computation | loop fusion | flops 1048576 | bytes 4194304 | tf_op jit(solution)/shard_map/concatenate | solution.py:27
  23.7 0.0 copy-start.6
  23.7 0.0 copy-start.7
  23.7 0.0 all-gather.2.cloned.1.call-update
  23.7 0.7 copy-done.6
  24.4 0.0 copy-done.7
  24.4 8.1 %all_gather.9 = bf16[2048,1]{0,1:T(2,128)(2,1)S(1)} all-gather(bf16[512,1]{0,1:T(2,128)(2,1)S(1)} %multiply_convert_fusion), channel_id=1, replica_groups=mesh['ep'=64,'fsdp'=4] {'fsdp'}, dimensions={0}, use_global_device_ids=true | all-gather | bytes 5120 | tf_op jit(solution)/shard_map/all_gather | solution.py:56
  32.6 0.3 broadcast_bitcast_fusion
  32.8 0.5 broadcast.9
  33.4 2.2 %reduce.4 = bf16[64,2048]{1,0:T(8,128)(2,1)S(1)} reduce(bf16[64,1,2048]{2,1,0:T(2,128)(2,1)S(1)} %broadcast_bitcast_fusion, bf16[]{:T(256)} %broadcast.9), dimensions={1}, to_apply=%broadcast_bitcast_fusion.reduce_sub_computation | reduce | bytes 524290
  35.5 0.2 reshape.38
  35.7 28.9 %all_to_all.12 = bf16[64,2,1024]{2,1,0:T(2,128)(2,1)S(1)} all-to-all(bf16[64,2,1024]{2,1,0:T(2,128)(2,1)S(1)} %reshape.38), channel_id=1, replica_groups=mesh['ep'=64,'fsdp'=4] {'ep'}, dimensions={0} | all-to-all | bytes 524288 | tf_op jit(solution)/shard_map/all_to_all | solution.py:9
  64.6 0.2 reshape.39
  64.9 0.9 copy.19
  65.7 46.1 %all-gather.2.cloned.1.call-done = bf16[2,2048,1024]{2,1,0:T(8,128)(2,1)} async-done(((bf16[2,512,1024]{2,1,0:T(8,128)(2,1)}), bf16[2,2048,1024]{2,1,0:T(8,128)(2,1)}) %all-gather.2.cloned.1.call-update) | async-done | bytes 8388624 | tf_op jit(solution)/shard_map/all_gather | solution.py:28
  111.8 6.0 %fusion = (bf16[1,2048,1024]{2,1,0:T(8,128)(2,1)}, bf16[1,2048,1024]{2,1,0:T(8,128)(2,1)}) fusion(bf16[2,2048,1024]{2,1,0:T(8,128)(2,1)} %all-gather.2.cloned.1.call-done), kind=kLoop, calls=%fused_computation.12 | loop fusion | bytes 16777216 | tf_op jit(solution)/shard_map/split | solution.py:29
  (6 shorter events, 0.1 us)
Async XLA Ops:
  7.2 12.7 %copy-start = (f32[1,512,1024]{2,1,0:T(8,128)S(1)}, f32[1,512,1024]{2,1,0:T(8,128)}, u32[]{:S(2)}) copy-start(f32[1,512,1024]{2,1,0:T(8,128)} %param.8) | copy-start | bytes 6291460
  7.2 12.7 %copy-start.2 = (bf16[1,512,1024]{2,1,0:T(8,128)(2,1)S(1)}, bf16[1,512,1024]{2,1,0:T(8,128)(2,1)}, u32[]{:S(2)}) copy-start(bf16[1,512,1024]{2,1,0:T(8,128)(2,1)} %param.9) | copy-start | bytes 3145732
  7.2 104.7 %all-gather.2.cloned.1.call-start = ((), (), s32[]{:S(2)}) async-start(), calls=%async_computation.2 | async-start | bytes 10485760 | tf_op jit(solution)/shard_map/all_gather | solution.py:28
  19.9 0.6 copy-start.5
  19.9 0.6 copy-start.4
  19.9 1.6 %copy-start.1 = (f32[1,512,1024]{2,1,0:T(8,128)S(1)}, f32[1,512,1024]{2,1,0:T(8,128)}, u32[]{:S(2)}) copy-start(f32[1,512,1024]{2,1,0:T(8,128)} %param.6) | copy-start | bytes 6291460
  19.9 1.8 %copy-start.3 = (bf16[1,512,1024]{2,1,0:T(8,128)(2,1)S(1)}, bf16[1,512,1024]{2,1,0:T(8,128)(2,1)}, u32[]{:S(2)}) copy-start(bf16[1,512,1024]{2,1,0:T(8,128)(2,1)} %param.7) | copy-start | bytes 3145732
  23.7 0.7 copy-start.6
  23.7 0.7 copy-start.7
Sparse Core Ops, SparseCore 0:
  23.8 87.9 all-gather.1
where the time goes:
time: 125 us
  waiting for transfers between devices  46.1 us (37%)
  blocking collectives  46 us (37%)
  between operations  14.2 us (11%)
  local copies, waits for them, and re-layouts  10.2 us (8%)
  other arithmetic  8.13 us (7%)
    all_gather x1, waiting for transfers between devices, side_by_side(): out = lax.all_gather(both, axis, axis=dim, tiled=True)  46.1 us
    all_to_all x2, blocking collectives, copy_for_each(): return lax.all_to_all(copies, axis, split_axis=0, concat_axis=0, tiled=True)  37.9 us
    all_gather x1, blocking collectives, body(): row_router = lax.all_gather(part_router, 'fsdp', axis=0, tiled=True)  8.13 us
    split x1, local copies, waits for them, and re-layouts, side_by_side(): jnp.split(out, [sum(widths[:k]) for k in range(1, len(widths))], axis=along)  6.02 us
    reduce_sum x1, other arithmetic, body(): jnp.sum(latest_up * latest_up, axis=1)  3.63 us
    unnamed x20, local copies, waits for them, and re-layouts  3.34 us
  transfers between devices with their start and end apart: 1, of which 1 were waited for; matrix products, arithmetic and copies ran while one was open for 3% of the time, Pallas kernels for 0%

commit v1 on v0

--- a/solution.py
+++ b/solution.py
@@ -2,6 +2,12 @@
 import jax.numpy as jnp
 from jax import lax
 from jax.sharding import PartitionSpec as P
+
+
+def in_order(blocks, dim):
+    blocks = jnp.moveaxis(blocks, 0, dim)
+    lengths = blocks.shape
+    return blocks.reshape(*lengths[:dim], lengths[dim] * lengths[dim + 1], *lengths[dim + 2 :])
 
 
 def copy_for_each(value, axis):
@@ -53,7 +59,19 @@
     )
     ready_gate, ready_up = side_by_side((narrow_gate, narrow_up), "fsdp", 1, 0)
     part_router = (router_weight * router_gain[:, None]).astype(jnp.bfloat16)
-    row_router = lax.all_gather(part_router, "fsdp", axis=0, tiled=True)
+    devices = lax.axis_size("fsdp")
+    pairs = [(i, (i + 1) % devices) for i in range(devices)]
+    back = [(b, a_2) for a_2, b in pairs]
+    lower, upper = ([], [])
+    for step in range(devices - 1):
+        if step % 2 == 0:
+            lower.append(lax.ppermute(lower[-1] if lower else part_router, "fsdp", pairs))
+        else:
+            upper.append(lax.ppermute(upper[-1] if upper else part_router, "fsdp", back))
+    blocks_2 = jnp.stack([*lower[::-1], part_router, *upper])
+    shift = lax.axis_index("fsdp") - len(lower)
+    blocks_2 = blocks_2[(jnp.arange(devices) - shift) % devices]
+    row_router = in_order(blocks_2, 0)
     serve_router = gather_directly(row_router, "ep", 1)
     return (ready_gate, ready_up, scale_gate, scale_up, serve_router)
 

time: 125 us -> 125 us (level)
  blocking collectives: 46 us -> 38.1 us
  waiting for transfers between devices: 46.1 us -> 51.9 us
  starting transfers between devices: 0.04 us -> 1.57 us
    all_gather x1 -> x0, blocking collectives: 8.13 us -> none  [body(): row_router = lax.all_gather(part_router, 'fsdp', axis=0, tiled=True)]
    ppermute x0 -> x3, waiting for transfers between devices: none -> 6.68 us  [the longest x2 6.68 us: body(): lax.ppermute(lower[-1] if lower else part_router, 'fsdp', pairs)]
    ppermute x0 -> x3, starting transfers between devices: none -> 1.53 us  [the longest x1 0.95 us: body(): lax.ppermute(upper[-1] if upper else part_router, 'fsdp', back)]
    unnamed x20 -> x21, local copies, waits for them, and re-layouts: 3.34 us -> 3.35 us
  transfers between devices with their start and end apart: 1 -> 4, of which waited for: 1 -> 3; matrix products, arithmetic and copies ran while one was open for 3% -> 4% of each run, Pallas kernels for 0% -> 0%
where the time goes in v1:
time: 125 us
  waiting for transfers between devices  51.9 us (42%)
  blocking collectives  38.1 us (30%)
  between operations  14.2 us (11%)
  local copies, waits for them, and re-layouts  10.8 us (9%)
  other arithmetic  8.13 us (7%)
  starting transfers between devices  1.57 us (1%)
    all_gather x1, waiting for transfers between devices, side_by_side(): out = lax.all_gather(both, axis, axis=dim, tiled=True)  45.2 us
    all_to_all x2, blocking collectives, copy_for_each(): return lax.all_to_all(copies, axis, split_axis=0, concat_axis=0, tiled=True)  38.1 us
    ppermute x2, waiting for transfers between devices, body(): lax.ppermute(lower[-1] if lower else part_router, 'fsdp', pairs)  6.68 us
    split x1, local copies, waits for them, and re-layouts, side_by_side(): jnp.split(out, [sum(widths[:k]) for k in range(1, len(widths))], axis=along)  6.02 us
    reduce_sum x1, other arithmetic, body(): jnp.sum(latest_up * latest_up, axis=1)  3.63 us
    unnamed x21, local copies, waits for them, and re-layouts  3.35 us
  transfers between devices with their start and end apart: 4, of which 3 were waited for; matrix products, arithmetic and copies ran while one was open for 4% of the time, Pallas kernels for 0%

profile of v1, /device:TPU:1, one launch (start us, length us, event | category | flops | bytes accessed | tf_op | source)
XLA Modules:
  0.0 124.7 jit_solution(10926996857640835054)
XLA Ops:
  7.2 0.0 copy-start
  7.2 0.0 copy-start.2
  7.2 0.0 all-gather.2.cloned.1.call-start
  7.2 3.6 %multiply_reduce_fusion = (f32[1024]{0:T(1024)S(1)}, f32[1024]{0:T(1024)S(1)}) fusion(f32[1,512,1024]{2,1,0:T(8,128)} %param.8, bf16[1,512,1024]{2,1,0:T(8,128)(2,1)} %param.9, f32[1,512,1024]{2,1,0:T(8,128)} %param.6, bf16[1,512,1024]{2,1,0:T(8,128)(2,1)} %param.7), kind=kLoop, calls=%fused_computation.4 | loop fusion | flops 4192256 | bytes 6299648 | tf_op jit(solution)/shard_map/reduce_sum | solution.py:52
  10.9 8.9 %all_to_all.11 = f32[4,1,2048]{2,1,0:T(1,128)S(1)} all-to-all(f32[4,1,2048]{2,1,0:T(1,128)S(1)} %broadcast_in_dim.12), channel_id=1, replica_groups=mesh['ep'=64,'fsdp'=4] {'fsdp'}, dimensions={0} | all-to-all | bytes 65536 | tf_op jit(solution)/shard_map/all_to_all | solution.py:15
  19.9 0.0 copy-start.5
  19.9 0.0 copy-start.4
  19.9 0.0 copy-done
  19.9 0.0 copy-done.2
  19.9 0.0 copy-start.1
  19.9 0.0 copy-start.3
  20.0 0.4 divide_convert_fusion
  20.3 0.1 copy-done.5
  20.5 0.0 copy-done.4
  20.5 1.0 copy-done.1
  21.5 0.3 copy-done.3
  21.8 0.4 divide_convert_fusion.1
  22.2 1.5 %pad_maximum_fusion = bf16[2,512,1024]{2,1,0:T(8,128)(2,1)} fusion(bf16[1,512,1024]{2,1,0:T(8,128)(2,1)S(1)} %divide_convert_fusion, bf16[1,512,1024]{2,1,0:T(8,128)(2,1)S(1)} %divide_convert_fusion.1), kind=kLoop, calls=%fused_computation.1 | loop fusion | flops 1048576 | bytes 4194304 | tf_op jit(solution)/shard_map/concatenate | solution.py:33
  23.7 0.0 copy-start.6
  23.7 0.0 copy-start.7
  23.7 0.0 all-gather.2.cloned.1.call-update
  23.7 0.7 copy-done.6
  24.4 0.0 copy-done.7
  24.4 0.9 collective-permute-start.2
  25.4 0.6 collective-permute-start
  25.9 3.1 %collective-permute-done = bf16[512,1]{0,1:T(2,128)(2,1)S(1)} collective-permute-done((bf16[512,1]{0,1:T(2,128)(2,1)S(1)}, bf16[512,1]{0,1:T(2,128)(2,1)S(1)}, u32[]{:S(2)}, u32[]{:S(2)}) %collective-permute-start) | collective-permute-done | bytes 1056 | tf_op jit(solution)/shard_map/ppermute | solution.py:68
  29.0 0.0 collective-permute-start.1
  29.0 0.0 collective-permute-done.2
  29.0 3.6 %collective-permute-done.1 = bf16[512,1]{0,1:T(2,128)(2,1)S(1)} collective-permute-done((bf16[512,1]{0,1:T(2,128)(2,1)S(1)}, bf16[512,1]{0,1:T(2,128)(2,1)S(1)}, u32[]{:S(2)}, u32[]{:S(2)}) %collective-permute-start.1) | collective-permute-done | bytes 1056 | tf_op jit(solution)/shard_map/ppermute | solution.py:68
  32.7 0.6 gather_fusion
  33.2 0.3 broadcast_bitcast_fusion
  33.5 0.5 broadcast.77
  34.0 2.2 %reduce.3 = bf16[64,2048]{1,0:T(8,128)(2,1)S(1)} reduce(bf16[64,1,2048]{2,1,0:T(2,128)(2,1)S(1)} %broadcast_bitcast_fusion, bf16[]{:T(256)} %broadcast.77), dimensions={1}, to_apply=%broadcast_bitcast_fusion.reduce_sub_computation | reduce | bytes 524290
  36.2 0.2 reshape.102
  36.4 29.2 %all_to_all.12 = bf16[64,2,1024]{2,1,0:T(2,128)(2,1)S(1)} all-to-all(bf16[64,2,1024]{2,1,0:T(2,128)(2,1)S(1)} %reshape.102), channel_id=1, replica_groups=mesh['ep'=64,'fsdp'=4] {'ep'}, dimensions={0} | all-to-all | bytes 524288 | tf_op jit(solution)/shard_map/all_to_all | solution.py:15
  65.6 0.2 reshape.103
  65.8 0.9 copy.20
  66.7 45.2 %all-gather.2.cloned.1.call-done = bf16[2,2048,1024]{2,1,0:T(8,128)(2,1)} async-done(((bf16[2,512,1024]{2,1,0:T(8,128)(2,1)}), bf16[2,2048,1024]{2,1,0:T(8,128)(2,1)}) %all-gather.2.cloned.1.call-update) | async-done | bytes 8388624 | tf_op jit(solution)/shard_map/all_gather | solution.py:34
  111.8 6.0 %fusion.2 = (bf16[1,2048,1024]{2,1,0:T(8,128)(2,1)}, bf16[1,2048,1024]{2,1,0:T(8,128)(2,1)}) fusion(bf16[2,2048,1024]{2,1,0:T(8,128)(2,1)} %all-gather.2.cloned.1.call-done), kind=kLoop, calls=%fused_computation.21 | loop fusion | bytes 16777216 | tf_op jit(solution)/shard_map/split | solution.py:35
  (9 shorter events, 0.1 us)
Async XLA Ops:
  7.2 12.7 %copy-start = (f32[1,512,1024]{2,1,0:T(8,128)S(1)}, f32[1,512,1024]{2,1,0:T(8,128)}, u32[]{:S(2)}) copy-start(f32[1,512,1024]{2,1,0:T(8,128)} %param.8) | copy-start | bytes 6291460
  7.2 12.7 %copy-start.2 = (bf16[1,512,1024]{2,1,0:T(8,128)(2,1)S(1)}, bf16[1,512,1024]{2,1,0:T(8,128)(2,1)}, u32[]{:S(2)}) copy-start(bf16[1,512,1024]{2,1,0:T(8,128)(2,1)} %param.9) | copy-start | bytes 3145732
  7.2 104.7 %all-gather.2.cloned.1.call-start = ((), (), s32[]{:S(2)}) async-start(), calls=%async_computation.2 | async-start | bytes 10485760 | tf_op jit(solution)/shard_map/all_gather | solution.py:34
  19.9 0.6 copy-start.5
  19.9 0.6 copy-start.4
  19.9 1.6 %copy-start.1 = (f32[1,512,1024]{2,1,0:T(8,128)S(1)}, f32[1,512,1024]{2,1,0:T(8,128)}, u32[]{:S(2)}) copy-start(f32[1,512,1024]{2,1,0:T(8,128)} %param.6) | copy-start | bytes 6291460
  19.9 1.8 %copy-start.3 = (bf16[1,512,1024]{2,1,0:T(8,128)(2,1)S(1)}, bf16[1,512,1024]{2,1,0:T(8,128)(2,1)}, u32[]{:S(2)}) copy-start(bf16[1,512,1024]{2,1,0:T(8,128)(2,1)} %param.7) | copy-start | bytes 3145732
  23.7 0.7 copy-start.6
  23.7 0.7 copy-start.7
  24.4 4.6 %collective-permute-start.2 = (bf16[512,1]{0,1:T(2,128)(2,1)S(1)}, bf16[512,1]{0,1:T(2,128)(2,1)S(1)}, u32[]{:S(2)}, u32[]{:S(2)}) collective-permute-start(bf16[512,1]{0,1:T(2,128)(2,1)S(1)} %multiply_convert_fusion), channel_id=1, source_target_pairs={{1,0},{2,1},{3,2},{0,3},{5,4},{6,5},{7,6},{4,7},{9,8},{10,9},{11,1... | collective-permute-start | bytes 3080 | tf_op jit(solution)/shard_map/ppermute | solution.py:70
  25.4 3.6 %collective-permute-start = (bf16[512,1]{0,1:T(2,128)(2,1)S(1)}, bf16[512,1]{0,1:T(2,128)(2,1)S(1)}, u32[]{:S(2)}, u32[]{:S(2)}) collective-permute-start(bf16[512,1]{0,1:T(2,128)(2,1)S(1)} %multiply_convert_fusion), channel_id=1, source_target_pairs={{0,1},{1,2},{2,3},{3,0},{4,5},{5,6},{6,7},{7,4},{8,9},{9,10},{10,1... | collective-permute-start | bytes 3080 | tf_op jit(solution)/shard_map/ppermute | solution.py:68
  29.0 3.6 %collective-permute-start.1 = (bf16[512,1]{0,1:T(2,128)(2,1)S(1)}, bf16[512,1]{0,1:T(2,128)(2,1)S(1)}, u32[]{:S(2)}, u32[]{:S(2)}) collective-permute-start(bf16[512,1]{0,1:T(2,128)(2,1)S(1)} %collective-permute-done), channel_id=1, source_target_pairs={{0,1},{1,2},{2,3},{3,0},{4,5},{5,6},{6,7},{7,4},{8,9},{9,10},{10,1... | collective-permute-start | bytes 3080 | tf_op jit(solution)/shard_map/ppermute | solution.py:68
Sparse Core Ops, SparseCore 0:
  23.8 87.9 all-gather.1
